TPU v7x, 768 devices: a whole 4x8x12 slice. The times are simulated.
768 devices in a mesh: lon: 32 (over x, z_hi, core), lat: 24 (over z_lo, y).
Axes of the slice: x: 4, y: 8, z: 12 (z_hi: 4, z_lo: 3; z = z_hi * 3 + z_lo), core: 2. Of those that a mesh axis runs over, the one named last changes fastest.
Arguments:
- fields: bfloat16 [144, 384, 2, 192], P('lat', 'lon'), may hold values from -6 to 6
- cotangent: bfloat16 [144, 384, 2, 192], P('lat', 'lon'), may hold values from -6 to 6
- qkv_plain: bfloat16 [192, 576], replicated, may hold values from -0.4375 to 0.4375
- proj_plain: bfloat16 [192, 192], replicated, may hold values from -0.4375 to 0.4375
- up_plain: bfloat16 [192, 768], replicated, may hold values from -0.4375 to 0.4375
- down_plain: bfloat16 [768, 192], replicated, may hold values from -0.21875 to 0.21875
- bias_plain: bfloat16 [24, 1, 6, 144, 144], P('lat'), may hold values from -4 to 4
- qkv_shift: bfloat16 [192, 576], replicated, may hold values from -0.4375 to 0.4375
- proj_shift: bfloat16 [192, 192], replicated, may hold values from -0.4375 to 0.4375
- up_shift: bfloat16 [192, 768], replicated, may hold values from -0.4375 to 0.4375
- down_shift: bfloat16 [768, 192], replicated, may hold values from -0.21875 to 0.21875
- bias_shift: bfloat16 [24, 1, 6, 144, 144], P('lat'), may hold values from -4 to 4
Outputs:
- result: bfloat16 [144, 384, 2, 192], P('lat', 'lon')
- grad_fields: bfloat16 [144, 384, 2, 192], P('lat', 'lon')
- grad_qkv_plain: float32 [192, 576], P(None, 'lat')
- grad_proj_plain: float32 [192, 192], P(None, 'lat')
- grad_up_plain: float32 [192, 768], P(None, 'lat')
- grad_down_plain: float32 [768, 192], P(None, 'lat')
- grad_qkv_shift: float32 [192, 576], P(None, 'lat')
- grad_proj_shift: float32 [192, 192], P(None, 'lat')
- grad_up_shift: float32 [192, 768], P(None, 'lat')
- grad_down_shift: float32 [768, 192], P(None, 'lat')
All inputs are finite; a program needn't handle non-finite values.
Results may differ from a plain program's by a relative error of at most 0.04.
Values may be sent and summed in bfloat16 or wider, within the bound.
No kernel may reach another device: no remote copies, remote signals or barrier semaphores. Data moves between devices by JAX's collectives and lax.ppermute only.
A program may use at most 64 MiB of HBM per device.

v0:
```python
import jax
import jax.numpy as jnp
from jax import lax
from jax.sharding import PartitionSpec as P

WLAT = 6
WLON = 12
WPL = 2


EPS = 1e-05


def shifted_2(value, axis, steps):
    count = lax.axis_size(axis)
    pairs = [(source, (source + steps) % count) for source in range(count)]
    return lax.ppermute(value, axis, pairs)


def in_blocks(x, dim, count):
    before, after = (x.shape[:dim], x.shape[dim + 1 :])
    return jnp.moveaxis(x.reshape(*before, count, -1, *after), dim, 0)


def one_scatter(arrays, axis, dims):
    count = lax.axis_size(axis)
    tiles = [in_blocks(a, dim, count) for a, dim in zip(arrays, dims)]
    lines = jnp.concatenate([b.reshape(count, -1) for b in tiles], axis=1)
    rows = max(16, -(-lines.shape[1] // 1024) * 8)
    lines = jnp.pad(lines, ((0, 0), (0, rows * 128 - lines.shape[1]))).reshape(-1, 128)
    ravelled, at, finished = (lax.psum_scatter(lines, axis, tiled=True).reshape(-1), 0, [])
    for b in tiles:
        part = b[0]
        finished.append(ravelled[at : at + part.size].reshape(part.shape))
        at += part.size
    return tuple(finished)


def normalize(values):
    average = jnp.mean(values, axis=-1, keepdims=True)
    centred = values - average
    variance = jnp.mean(centred * centred, axis=-1, keepdims=True)
    return centred * lax.rsqrt(variance + EPS)


def to_windows(grid):
    lat_cells, lon_cells, levels = grid.shape[:3]
    trailing = grid.shape[3:]
    blocked = grid.reshape(
        (lat_cells // WLAT, WLAT, lon_cells // WLON, WLON, levels // WPL, WPL) + trailing
    )
    ordering = (0, 2, 4, 1, 3, 5) + tuple(range(6, 6 + len(trailing)))
    permuted = jnp.transpose(blocked, ordering)
    return permuted.reshape(
        (lat_cells // WLAT, lon_cells // WLON * (levels // WPL), WLAT * WLON * WPL) + trailing
    )


def from_windows(wins, lat_cells, lon_cells, levels):
    trailing = wins.shape[3:]
    blocked = wins.reshape(
        (lat_cells // WLAT, lon_cells // WLON, levels // WPL, WLAT, WLON, WPL) + trailing
    )
    ordering = (0, 3, 1, 4, 2, 5) + tuple(range(6, 6 + len(trailing)))
    permuted = jnp.transpose(blocked, ordering)
    return permuted.reshape((lat_cells, lon_cells, levels) + trailing)


def block_forward(inputs, weights, bias, groups):
    w_qkv, w_proj, w_up, w_down = weights
    bands, per_band, window_size, width = inputs.shape
    pressure_wins = bias.shape[1]
    heads = bias.shape[2]
    head_size = width // heads
    flat_in = inputs.reshape(-1, width).astype(jnp.float32)
    normed = normalize(flat_in).astype(jnp.bfloat16)
    mixed = jnp.dot(normed, w_qkv, preferred_element_type=jnp.float32).astype(jnp.bfloat16)
    mixed = mixed.reshape(bands, per_band, window_size, 3, heads, head_size)
    query_part = mixed[:, :, :, 0]
    key_part = mixed[:, :, :, 1]
    value_part = mixed[:, :, :, 2]
    scores = jnp.einsum(
        "bnqhd,bnkhd->bnhqk", query_part, key_part, preferred_element_type=jnp.float32
    )
    scores = scores.reshape(
        bands, per_band // pressure_wins, pressure_wins, heads, window_size, window_size
    )
    scores = scores * head_size ** (-0.5) + bias[:, None].astype(jnp.float32)
    scores = scores.reshape(bands, per_band, heads, window_size, window_size)
    allowed = (groups[:, :, :, None] == groups[:, :, None, :])[:, :, None].astype(jnp.float32)
    weighted = jnp.exp(scores) * allowed
    probs = weighted / jnp.sum(weighted, axis=-1, keepdims=True)
    probs_low = probs.astype(jnp.bfloat16)
    attended = jnp.einsum(
        "bnhqk,bnkhd->bnqhd", probs_low, value_part, preferred_element_type=jnp.float32
    )
    attended = attended.astype(jnp.bfloat16).reshape(-1, width)
    after_attn = (flat_in + jnp.dot(attended, w_proj, preferred_element_type=jnp.float32)).astype(
        jnp.bfloat16
    )
    after_f32 = after_attn.astype(jnp.float32)
    normed_two = normalize(after_f32).astype(jnp.bfloat16)
    pre_act = jnp.dot(normed_two, w_up, preferred_element_type=jnp.float32)
    activated = jax.nn.gelu(pre_act).astype(jnp.bfloat16)
    outputs = (after_f32 + jnp.dot(activated, w_down, preferred_element_type=jnp.float32)).astype(
        jnp.bfloat16
    )
    saved = (
        flat_in,
        normed,
        query_part,
        key_part,
        value_part,
        probs,
        probs_low,
        attended,
        after_f32,
        normed_two,
        pre_act,
        activated,
    )
    return (outputs.reshape(inputs.shape), saved)


def block_backward(saved, cotangent, weights):
    w_qkv, w_proj, w_up, w_down = weights
    (
        flat_in,
        normed,
        query_part,
        key_part,
        value_part,
        probs,
        probs_low,
        attended,
        after_f32,
        normed_two,
        pre_act,
        activated,
    ) = saved
    width = flat_in.shape[1]
    scale = query_part.shape[-1] ** (-0.5)
    grad_out = cotangent.reshape(-1, width)
    grad_down = jnp.dot(activated.T, grad_out, preferred_element_type=jnp.float32)
    grad_act = jnp.dot(grad_out, w_down.T, preferred_element_type=jnp.float32)
    unused_one, gelu_back = jax.vjp(jax.nn.gelu, pre_act)
    grad_pre = gelu_back(grad_act)[0].astype(jnp.bfloat16)
    grad_up = jnp.dot(normed_two.T, grad_pre, preferred_element_type=jnp.float32)
    grad_norm_two = jnp.dot(grad_pre, w_up.T, preferred_element_type=jnp.float32)
    unused_two, second_back = jax.vjp(normalize, after_f32)
    grad_after = grad_out.astype(jnp.float32) + second_back(grad_norm_two)[0]
    grad_after_low = grad_after.astype(jnp.bfloat16)
    grad_proj = jnp.dot(attended.T, grad_after_low, preferred_element_type=jnp.float32)
    grad_attended = jnp.dot(grad_after_low, w_proj.T, preferred_element_type=jnp.float32).astype(
        jnp.bfloat16
    )
    grad_attended = grad_attended.reshape(query_part.shape)
    grad_value = jnp.einsum(
        "bnhqk,bnqhd->bnkhd", probs_low, grad_attended, preferred_element_type=jnp.float32
    ).astype(jnp.bfloat16)
    grad_probs = jnp.einsum(
        "bnqhd,bnkhd->bnhqk", grad_attended, value_part, preferred_element_type=jnp.float32
    )
    grad_scores = (
        probs * (grad_probs - jnp.sum(grad_probs * probs, axis=-1, keepdims=True)) * scale
    ).astype(jnp.bfloat16)
    grad_query = jnp.einsum(
        "bnhqk,bnkhd->bnqhd", grad_scores, key_part, preferred_element_type=jnp.float32
    ).astype(jnp.bfloat16)
    grad_key = jnp.einsum(
        "bnhqk,bnqhd->bnkhd", grad_scores, query_part, preferred_element_type=jnp.float32
    ).astype(jnp.bfloat16)
    grad_mixed = jnp.stack([grad_query, grad_key, grad_value], axis=3).reshape(-1, 3 * width)
    grad_qkv = jnp.dot(normed.T, grad_mixed, preferred_element_type=jnp.float32)
    grad_normed = jnp.dot(grad_mixed, w_qkv.T, preferred_element_type=jnp.float32)
    unused_three, first_back = jax.vjp(normalize, flat_in)
    grad_in = (grad_after + first_back(grad_normed)[0]).astype(jnp.bfloat16)
    return (grad_in.reshape(cotangent.shape), (grad_qkv, grad_proj, grad_up, grad_down))


def move_frame(field, forward):
    lat_half = WLAT // 2
    lon_half = WLON // 2
    offset = -1 if forward else 1
    border = field[:lat_half] if forward else field[-lat_half:]
    lat_piece = shifted_2(border, "lat", offset)
    if forward:
        widened = jnp.concatenate([field[lat_half:], lat_piece], axis=0)
    else:
        widened = jnp.concatenate([lat_piece, field[:-lat_half]], axis=0)
    border_cols = widened[:, :lon_half] if forward else widened[:, -lon_half:]
    lon_piece = shifted_2(border_cols, "lon", offset)
    if forward:
        shifted = jnp.concatenate([widened[:, lon_half:], lon_piece], axis=1)
    else:
        shifted = jnp.concatenate([lon_piece, widened[:, :-lon_half]], axis=1)
    return jnp.roll(shifted, (-1 if forward else 1) * (WPL // 2), axis=2)


def reduce_all(grads):
    shares = tuple(
        (
            part.astype(jnp.float32)
            for part in one_scatter(
                (
                    grads[0].astype(jnp.bfloat16),
                    grads[1].astype(jnp.bfloat16),
                    grads[2].astype(jnp.bfloat16),
                    grads[3].astype(jnp.bfloat16),
                    grads[4].astype(jnp.bfloat16),
                    grads[5].astype(jnp.bfloat16),
                    grads[6].astype(jnp.bfloat16),
                    grads[7].astype(jnp.bfloat16),
                ),
                "lat",
                (1, 1, 1, 1, 1, 1, 1, 1),
            )
        )
    )
    return (
        lax.psum(shares[0].astype(jnp.bfloat16), "lon").astype(jnp.float32),
        lax.psum(shares[1].astype(jnp.bfloat16), "lon").astype(jnp.float32),
        lax.psum(shares[2].astype(jnp.bfloat16), "lon").astype(jnp.float32),
        lax.psum(shares[3].astype(jnp.bfloat16), "lon").astype(jnp.float32),
        lax.psum(shares[4].astype(jnp.bfloat16), "lon").astype(jnp.float32),
        lax.psum(shares[5].astype(jnp.bfloat16), "lon").astype(jnp.float32),
        lax.psum(shares[6].astype(jnp.bfloat16), "lon").astype(jnp.float32),
        lax.psum(shares[7].astype(jnp.bfloat16), "lon").astype(jnp.float32),
    )


def local(
    fields,
    cotangent,
    qkv_plain,
    proj_plain,
    up_plain,
    down_plain,
    bias_plain,
    qkv_shift,
    proj_shift,
    up_shift,
    down_shift,
    bias_shift,
):
    lat_cells, lon_cells, levels = fields.shape[:3]
    plain = (qkv_plain, proj_plain, up_plain, down_plain)
    shifted = (qkv_shift, proj_shift, up_shift, down_shift)
    total_lat = lat_cells * lax.axis_size("lat")
    lat_index = lax.axis_index("lat") * lat_cells + jnp.arange(lat_cells, dtype=jnp.int32)
    level_index = jnp.arange(levels, dtype=jnp.int32)
    group_shift = (lat_index >= total_lat - WLAT // 2).astype(jnp.int32)[:, None, None] * 2 + (
        level_index >= levels - WPL // 2
    ).astype(jnp.int32)[None, None, :]
    group_shift = jnp.broadcast_to(group_shift, (lat_cells, lon_cells, levels))
    group_plain = jnp.zeros((lat_cells, lon_cells, levels), jnp.int32)
    first_out, saved_plain = block_forward(
        to_windows(fields), plain, bias_plain, to_windows(group_plain)
    )
    moved_in = move_frame(from_windows(first_out, lat_cells, lon_cells, levels), True)
    second_out, saved_shift = block_forward(
        to_windows(moved_in), shifted, bias_shift, to_windows(group_shift)
    )
    result = move_frame(from_windows(second_out, lat_cells, lon_cells, levels), False)
    moved_cot = move_frame(cotangent, True)
    grad_moved, grads_shift = block_backward(saved_shift, to_windows(moved_cot), shifted)
    grad_first = move_frame(from_windows(grad_moved, lat_cells, lon_cells, levels), False)
    grad_wins, grads_plain = block_backward(saved_plain, to_windows(grad_first), plain)
    grad_fields = from_windows(grad_wins, lat_cells, lon_cells, levels)
    summed = reduce_all(tuple(grads_plain) + tuple(grads_shift))
    tokens_total = lat_cells * lon_cells * levels * lax.axis_size("lat") * lax.axis_size("lon")
    factor = float(tokens_total) ** (-0.5)
    return (
        result,
        grad_fields,
        summed[0] * factor,
        summed[1] * factor,
        summed[2] * factor,
        summed[3] * factor,
        summed[4] * factor,
        summed[5] * factor,
        summed[6] * factor,
        summed[7] * factor,
    )


def solution(mesh):
    placed = (
        P("lat", "lon", None, None),
        P("lat", "lon", None, None),
        P(),
        P(),
        P(),
        P(),
        P("lat", None, None, None, None),
        P(),
        P(),
        P(),
        P(),
        P("lat", None, None, None, None),
    )
    return jax.shard_map(
        local,
        mesh=mesh,
        in_specs=placed,
        out_specs=(
            P("lat", "lon", None, None),
            P("lat", "lon", None, None),
            P(None, "lat"),
            P(None, "lat"),
            P(None, "lat"),
            P(None, "lat"),
            P(None, "lat"),
            P(None, "lat"),
            P(None, "lat"),
            P(None, "lat"),
        ),
        check_vma=False,
    )
```

profile of v0, /device:TPU:1, one launch (start us, length us, event | category | flops | bytes accessed | tf_op | source)
XLA Modules:
  0.0 598.4 jit_solution(356703498679211254)
XLA Ops:
  7.2 1.5 fusion.108
  8.8 9.5 %collective-permute-start.4 = (bf16[3,12,2,192]{3,2,1,0:T(2,128)(2,1)}, bf16[3,12,2,192]{3,2,1,0:T(2,128)(2,1)}, u32[]{:S(2)}, u32[]{:S(2)}) collective-permute-start(bf16[3,12,2,192]{3,2,1,0:T(2,128)(2,1)} %get-tuple-element.53), channel_id=1, source_target_pairs={{0,23},{1,0},{2,1},{3,2},{4,3},{5,4},{6,5},{7,6},{8,7},{9,8},{10,9... | collective-permute-start | bytes 82952 | tf_op jit(solution)/shard_map/ppermute | solution.py:17
  18.3 1.0 convert_reduce_fusion.1
  19.5 1.2 multiply_reduce_fusion.9
  22.4 1.2 convolution_convert_fusion.7
  26.8 3.0 collective-permute-start
  31.1 1.0 copy.46
  33.1 5.5 collective-permute-start.1
  39.5 11.5 %collective-permute-start.5 = (bf16[6,6,2,192]{3,2,1,0:T(2,128)(2,1)S(1)}, bf16[6,6,2,192]{3,2,1,0:T(2,128)(2,1)S(1)}, u32[]{:S(2)}, u32[]{:S(2)}) collective-permute-start(bf16[6,6,2,192]{3,2,1,0:T(2,128)(2,1)S(1)} %get-tuple-element.51), channel_id=1, source_target_pairs={{0,744},{24,0},{48,24},{72,48},{96,72},{120,96},{144,120},{168,144... | collective-permute-start | bytes 82952 | tf_op jit(solution)/shard_map/ppermute | solution.py:17
  54.4 1.6 fusion.56
  56.0 1.1 convolution_convert_fusion.14
  57.1 1.2 fusion.114
  60.4 1.1 convolution_convert_fusion.1
  63.4 1.6 copy.48
  65.0 1.8 fusion.27
  66.8 2.2 fusion.70
  69.0 2.4 fusion.25
  71.4 2.4 fusion.26
  74.8 1.1 pad_maximum_fusion
  76.2 1.2 convolution_convert_fusion.4
  77.8 1.0 add_convert_fusion.1
  78.8 2.3 collective-permute-start.6
  81.1 2.0 fusion.16
  83.2 3.3 collective-permute-done.6
  87.3 2.1 collective-permute-start.7
  92.2 2.0 reshape.619
  94.2 1.5 copy.63
  95.7 2.8 reshape.615
  98.4 2.2 copy.67
  100.6 1.3 copy.71
  101.9 1.0 slice_maximum_fusion
  103.9 1.5 fusion.47
  105.5 1.0 fusion.15
  108.8 1.0 fusion.28
  109.8 1.0 fusion.29
  111.3 1.0 pad_maximum_fusion.1
  113.3 2.0 reshape.611
  115.8 2.7 reshape.607
  118.6 1.1 copy.61
  120.4 1.7 constant_dynamic-update-slice_fusion.13
  122.7 1.7 constant_dynamic-update-slice_fusion.11
  128.0 3.9 reshape.622
  133.4 1.9 collective-permute-start.2
  135.3 5.8 collective-permute-done.2
  141.2 6.9 %collective-permute-start.3 = (bf16[6,6,2,192]{3,2,1,0:T(2,128)(2,1)S(1)}, bf16[6,6,2,192]{3,2,1,0:T(2,128)(2,1)S(1)}, u32[]{:S(2)}, u32[]{:S(2)}) collective-permute-start(bf16[6,6,2,192]{3,2,1,0:T(2,128)(2,1)S(1)} %get-tuple-element.54), channel_id=1, source_target_pairs={{0,24},{24,48},{48,72},{72,96},{96,120},{120,144},{144,168},{168,1... | collective-permute-start | bytes 82952 | tf_op jit(solution)/shard_map/ppermute | solution.py:17
  149.7 80.4 %reduce-scatter.2.cloned.1.call-done = bf16[288,128]{1,0:T(8,128)(2,1)} async-done(((bf16[6912,128]{1,0:T(8,128)(2,1)}), bf16[288,128]{1,0:T(8,128)(2,1)}) %reduce-scatter.2.cloned.1.call-update) | async-done | bytes 73744 | tf_op jit(solution)/shard_map/reduce_scatter | solution.py:31
  239.4 343.0 %all-reduce.3.cloned.1.call-done = (bf16[192,24]{1,0:T(8,128)(2,1)}, bf16[192,8]{1,0:T(8,128)(2,1)}, bf16[192,32]{1,0:T(8,128)(2,1)}, bf16[768,8]{1,0:T(8,128)(2...) async-done(((bf16[192,24]{1,0:T(8,128)(2,1)}, bf16[192,8]{1,0:T(8,128)(2,1)}, ...) | async-done | bytes 73744 | tf_op jit(solution)/shard_map/psum | solution.py:221
  589.0 1.1 convert_multiply_fusion
  (246 shorter events, 50.7 us)
Async XLA Ops:
  7.2 51.4 %copy-start = (bf16[192,768]{1,0:T(8,128)(2,1)S(1)}, bf16[192,768]{1,0:T(8,128)(2,1)}, u32[]{:S(2)}) copy-start(bf16[192,768]{1,0:T(8,128)(2,1)} %param.21) | copy-start | bytes 884740
  7.2 16.6 %copy-start.21 = (bf16[1,1,6,144,144]{4,3,2,1,0:T(8,128)(2,1)S(1)}, bf16[1,1,6,144,144]{4,3,2,1,0:T(8,128)(2,1)}, u32[]{:S(2)}) copy-start(bf16[1,1,6,144,144]{4,3,2,1,0:T(8,128)(2,1)} %param.18) | copy-start | bytes 746500
  7.2 222.9 %reduce-scatter.2.cloned.1.call-start = ((), (), s32[]{:S(2)}) async-start(), calls=%async_computation.1 | async-start | bytes 1843200 | tf_op jit(solution)/shard_map/reduce_scatter | solution.py:31
  8.8 29.8 %collective-permute-start.4 = (bf16[3,12,2,192]{3,2,1,0:T(2,128)(2,1)}, bf16[3,12,2,192]{3,2,1,0:T(2,128)(2,1)}, u32[]{:S(2)}, u32[]{:S(2)}) collective-permute-start(bf16[3,12,2,192]{3,2,1,0:T(2,128)(2,1)} %get-tuple-element.53), channel_id=1, source_target_pairs={{0,23},{1,0},{2,1},{3,2},{4,3},{5,4},{6,5},{7,6},{8,7},{9,8},{10,9... | collective-permute-start | bytes 82952 | tf_op jit(solution)/shard_map/ppermute | solution.py:17
  22.4 2.2 copy-start.34
  24.8 5.6 copy-start.8
  24.8 5.2 copy-start.4
  25.3 5.9 copy-start.22
  25.5 4.3 copy-start.40
  25.8 13.7 %copy-start.23 = (f32[144,768]{1,0:T(8,128)}, f32[144,768]{1,0:T(8,128)S(1)}, u32[]{:S(2)}) copy-start(f32[144,768]{1,0:T(8,128)S(1)} %fusion.96) | copy-start | bytes 1327108
  25.8 12.8 %copy-start.33 = (bf16[3,12,2,192]{3,2,1,0:T(2,128)(2,1)S(1)}, bf16[3,12,2,192]{3,2,1,0:T(2,128)(2,1)}, u32[]{:S(2)}) copy-start(bf16[3,12,2,192]{3,2,1,0:T(2,128)(2,1)} %get-tuple-element.52) | copy-start | bytes 82948
  26.8 5.4 collective-permute-start
  30.0 23.2 %copy-start.6 = (bf16[192,576]{1,0:T(8,128)(2,1)S(1)}, bf16[192,576]{1,0:T(8,128)(2,1)}, u32[]{:S(2)}) copy-start(bf16[192,576]{1,0:T(8,128)(2,1)} %param.19) | copy-start | bytes 663556
  33.1 17.9 %collective-permute-start.1 = (bf16[6,6,2,192]{3,2,1,0:T(2,128)(2,1)S(1)}, bf16[6,6,2,192]{3,2,1,0:T(2,128)(2,1)S(1)}, u32[]{:S(2)}, u32[]{:S(2)}) collective-permute-start(bf16[6,6,2,192]{3,2,1,0:T(2,128)(2,1)S(1)} %get-tuple-element.59), channel_id=1, source_target_pairs={{0,744},{24,0},{48,24},{72,48},{96,72},{120,96},{144,120},{168,144... | collective-permute-start | bytes 82952 | tf_op jit(solution)/shard_map/ppermute | solution.py:17
  39.5 12.5 %collective-permute-start.5 = (bf16[6,6,2,192]{3,2,1,0:T(2,128)(2,1)S(1)}, bf16[6,6,2,192]{3,2,1,0:T(2,128)(2,1)S(1)}, u32[]{:S(2)}, u32[]{:S(2)}) collective-permute-start(bf16[6,6,2,192]{3,2,1,0:T(2,128)(2,1)S(1)} %get-tuple-element.51), channel_id=1, source_target_pairs={{0,744},{24,0},{48,24},{72,48},{96,72},{120,96},{144,120},{168,144... | collective-permute-start | bytes 82952 | tf_op jit(solution)/shard_map/ppermute | solution.py:17
  53.2 2.8 copy-start.44
  53.2 2.8 copy-start.36
  56.0 3.7 copy-start.17
  56.0 3.7 copy-start.47
  57.1 2.9 copy-start.10
  60.1 2.5 copy-start.27
  61.8 9.6 %copy-start.38 = (f32[144]{0:T(256)}, f32[144]{0:T(256)S(1)}, u32[]{:S(2)}) copy-start(f32[144]{0:T(256)S(1)} %negate_multiply_fusion.3) | copy-start | bytes 1732
  73.8 3.7 copy-start.45
  73.8 3.7 copy-start.37
  73.8 3.9 copy-start.39
  74.1 7.1 %copy-start.18 = (bf16[144,192]{1,0:T(8,128)(2,1)S(1)}, bf16[144,192]{1,0:T(8,128)(2,1)}, u32[]{:S(2)}) copy-start(bf16[144,192]{1,0:T(8,128)(2,1)} %reshape_reshape_transpose_reshape.8) | copy-start | bytes 165892
  76.2 13.2 %copy-start.11 = (bf16[6,32,144]{2,1,0:T(8,128)(2,1)S(1)}, bf16[6,32,144]{2,1,0:T(8,128)(2,1)}, u32[]{:S(2)}) copy-start(bf16[6,32,144]{2,1,0:T(8,128)(2,1)} %copy-done.10) | copy-start | bytes 165892
  76.2 13.2 %copy-start.20 = (bf16[144,192]{1,0:T(8,128)(2,1)S(1)}, bf16[144,192]{1,0:T(8,128)(2,1)}, u32[]{:S(2)}) copy-start(bf16[144,192]{1,0:T(8,128)(2,1)} %copy-done.19) | copy-start | bytes 165892
  76.2 13.4 %copy-start.5 = (bf16[192,768]{1,0:T(8,128)(2,1)S(1)}, bf16[192,768]{1,0:T(8,128)(2,1)}, u32[]{:S(2)}) copy-start(bf16[192,768]{1,0:T(8,128)(2,1)} %convolution_convert_fusion.1) | copy-start | bytes 884740
  78.8 7.7 %collective-permute-start.6 = (bf16[3,12,2,192]{3,2,1,0:T(2,128)(2,1)S(1)}, bf16[3,12,2,192]{3,2,1,0:T(2,128)(2,1)S(1)}, u32[]{:S(2)}, u32[]{:S(2)}) collective-permute-start(bf16[3,12,2,192]{3,2,1,0:T(2,128)(2,1)S(1)} %slice.173), channel_id=1, source_target_pairs={{0,1},{1,2},{2,3},{3,4},{4,5},{5,6},{6,7},{7,8},{8,9},{9,10},{10,1... | collective-permute-start | bytes 82952 | tf_op jit(solution)/shard_map/ppermute | solution.py:17
  87.3 14.7 %collective-permute-start.7 = (bf16[6,6,2,192]{3,2,1,0:T(2,128)(2,1)}, bf16[6,6,2,192]{3,2,1,0:T(2,128)(2,1)}, u32[]{:S(2)}, u32[]{:S(2)}) collective-permute-start(bf16[6,6,2,192]{3,2,1,0:T(2,128)(2,1)} %get-tuple-element.46), channel_id=1, source_target_pairs={{0,24},{24,48},{48,72},{72,96},{96,120},{120,144},{144,168},{168,1... | collective-permute-start | bytes 82952 | tf_op jit(solution)/shard_map/ppermute | solution.py:17
  101.9 3.5 copy-start.24
  103.9 3.6 copy-start.15
  105.5 2.2 copy-start.9
  105.5 2.4 copy-start.29
  109.8 2.6 copy-start.30
  115.3 3.3 copy-start.31
  119.7 6.2 %copy-start.32 = (bf16[24,1536]{1,0:T(8,128)(2,1)S(1)}, bf16[24,1536]{1,0:T(8,128)(2,1)}, u32[]{:S(2)}) copy-start(bf16[24,1536]{1,0:T(8,128)(2,1)} %copy.70) | copy-start | bytes 221188
  120.4 4.8 copy-start.12
  120.4 6.2 %copy-start.3 = (bf16[24,6144]{1,0:T(8,128)(2,1)S(1)}, bf16[24,6144]{1,0:T(8,128)(2,1)}, u32[]{:S(2)}) copy-start(bf16[24,6144]{1,0:T(8,128)(2,1)} %reshape.619) | copy-start | bytes 884740
  120.4 6.9 %copy-start.2 = (bf16[24,6144]{1,0:T(8,128)(2,1)S(1)}, bf16[24,6144]{1,0:T(8,128)(2,1)}, u32[]{:S(2)}) copy-start(bf16[24,6144]{1,0:T(8,128)(2,1)} %copy.71) | copy-start | bytes 884740
  131.9 16.2 %copy-start.7 = (bf16[192,576]{1,0:T(8,128)(2,1)S(1)}, bf16[192,576]{1,0:T(8,128)(2,1)}, u32[]{:S(2)}) copy-start(bf16[192,576]{1,0:T(8,128)(2,1)} %param.14) | copy-start | bytes 663556
  132.0 16.5 %copy-start.43 = (f32[144]{0:T(256)S(1)}, f32[144]{0:T(256)}, u32[]{:S(2)}) copy-start(f32[144]{0:T(256)} %copy-done.42) | copy-start | bytes 1732
  132.0 16.5 %copy-start.35 = (f32[144]{0:T(256)S(1)}, f32[144]{0:T(256)}, u32[]{:S(2)}) copy-start(f32[144]{0:T(256)} %copy-done.34) | copy-start | bytes 1732
  132.0 16.8 %copy-start.16 = (bf16[144,192]{1,0:T(8,128)(2,1)S(1)}, bf16[144,192]{1,0:T(8,128)(2,1)}, u32[]{:S(2)}) copy-start(bf16[144,192]{1,0:T(8,128)(2,1)} %copy-done.15) | copy-start | bytes 165892
  132.0 450.3 %all-reduce.3.cloned.1.call-start = ((), (), s32[]{:S(2)}) async-start(), calls=%async_computation.2 | async-start | bytes 1376256 | tf_op jit(solution)/shard_map/psum | solution.py:221
  133.4 7.7 %collective-permute-start.2 = (bf16[3,12,2,192]{3,2,1,0:T(2,128)(2,1)S(1)}, bf16[3,12,2,192]{3,2,1,0:T(2,128)(2,1)S(1)}, u32[]{:S(2)}, u32[]{:S(2)}) collective-permute-start(bf16[3,12,2,192]{3,2,1,0:T(2,128)(2,1)S(1)} %slice.159), channel_id=1, source_target_pairs={{0,1},{1,2},{2,3},{3,4},{4,5},{5,6},{6,7},{7,8},{8,9},{9,10},{10,1... | collective-permute-start | bytes 82952 | tf_op jit(solution)/shard_map/ppermute | solution.py:17
  141.2 8.3 %collective-permute-start.3 = (bf16[6,6,2,192]{3,2,1,0:T(2,128)(2,1)S(1)}, bf16[6,6,2,192]{3,2,1,0:T(2,128)(2,1)S(1)}, u32[]{:S(2)}, u32[]{:S(2)}) collective-permute-start(bf16[6,6,2,192]{3,2,1,0:T(2,128)(2,1)S(1)} %get-tuple-element.54), channel_id=1, source_target_pairs={{0,24},{24,48},{48,72},{72,96},{96,120},{120,144},{144,168},{168,1... | collective-permute-start | bytes 82952 | tf_op jit(solution)/shard_map/ppermute | solution.py:17
  (11 other events, 11.3 us)
Sparse Core Ops, SparseCore 0:
  132.1 97.9 reduce-scatter.1
  238.7 343.6 all-reduce.2
where the time goes:
time: 600 us; the launch traced here: 598 us
  waiting for transfers between devices  433 us (72%)
  local copies, waits for them, and re-layouts  62 us (10%)
  starting transfers between devices  42.7 us (7%)
  matrix products  29.7 us (5%)
  other arithmetic  16.1 us (3%)
  between operations  15.3 us (3%)
    psum x1, waiting for transfers between devices, reduce_all(): lax.psum(shares[0].astype(jnp.bfloat16), 'lon').astype(jnp.float32)  343 us
    reduce_scatter x1, waiting for transfers between devices, one_scatter(): lax.psum_scatter(lines, axis, tiled=True).reshape(-1)  80.4 us
    ppermute x8, starting transfers between devices, shifted_2(): return lax.ppermute(value, axis, pairs)  42.7 us
    unnamed x118, local copies, waits for them, and re-layouts  17.2 us
    reshape x8, local copies, waits for them, and re-layouts, one_scatter(): lines = jnp.concatenate([b.reshape(count, -1) for b in tiles], axis=1)  12.3 us
  transfers between devices with their start and end apart: 10, of which 4 were waited for; matrix products, arithmetic and copies ran while one was open for 5% of the time, Pallas kernels for 0%

commit v1 on v0

v1 whole, which is shorter than its diff:
```python
import functools

import jax
import jax.numpy as jnp
import numpy as np
from jax import lax
from jax.experimental import pallas as pl
from jax.experimental.pallas import tpu as pltpu
from jax.sharding import PartitionSpec as P

WLAT = 6
WLON = 12
WPL = 2
WIN = WLAT * WLON * WPL
HEADS = 6
D = 192
HEAD = D // HEADS
FF = 768
PIECE = 40
EPS = 1e-05
F32 = jnp.float32
BF16 = jnp.bfloat16
VMEM = pl.BlockSpec(memory_space=pltpu.VMEM)
SMEM = pl.BlockSpec(memory_space=pltpu.SMEM)


def placements():
    half_lat, half_lon = WLAT // 2, WLON // 2

    def at(i, j, l):
        return (i * WLON + j) * WPL + l

    own = np.zeros((WIN, WIN), np.float32)
    take = np.zeros((3, PIECE, WIN), np.float32)
    put = np.zeros((3, WIN, PIECE), np.float32)
    corners = (
        (half_lat, 0, 0, half_lon),
        (0, half_lon, half_lat, 0),
        (half_lat, half_lon, 0, 0),
    )
    for i in range(half_lat):
        for j in range(half_lon):
            for l in range(WPL):
                own[at(i, j, 1 - l), at(i + half_lat, j + half_lon, l)] = 1
                row = (i * half_lon + j) * WPL + l
                for k, (di, dj, si, sj) in enumerate(corners):
                    take[k, row, at(i + si, j + sj, l)] = 1
                    put[k, at(i + di, j + dj, 1 - l), row] = 1
    return own, take, put


OWN, TAKE, PUT = placements()


def dot(a, b, dims=((1,), (0,))):
    return lax.dot_general(a, b, (dims, ((), ())), preferred_element_type=F32)


def dot_nt(a, b):
    return dot(a, b, ((1,), (1,)))


def dot_tn(a, b):
    return dot(a, b, ((0,), (0,)))


def normalize(values):
    average = jnp.mean(values, axis=-1, keepdims=True)
    centred = values - average
    variance = jnp.mean(centred * centred, axis=-1, keepdims=True)
    inverse = lax.rsqrt(variance + EPS)
    return centred * inverse, inverse


def normalize_back(normed, inverse, grad):
    mean_grad = jnp.mean(grad, axis=-1, keepdims=True)
    mean_both = jnp.mean(grad * normed, axis=-1, keepdims=True)
    return inverse * (grad - mean_grad - normed * mean_both)


GELU_A = np.float32(np.sqrt(2 / np.pi))
GELU_B = np.float32(0.044715)


def head_masks():
    lanes = lax.broadcasted_iota(jnp.int32, (WIN, D), 1)
    return [(lanes >= h * HEAD) & (lanes < (h + 1) * HEAD) for h in range(HEADS)]


def spread(values, masks):
    zero = jnp.zeros_like(values)
    return jnp.concatenate([jnp.where(m, values, zero) for m in masks], axis=0)


def gather_heads(stacked, masks):
    total = None
    for h, m in enumerate(masks):
        part = jnp.where(m, stacked[h * WIN : (h + 1) * WIN], 0.0)
        total = part if total is None else total + part
    return total


def forward(x, w_qkv, w_proj, w_up, w_down, bias, allowed):
    masks = head_masks()
    x32 = x.astype(F32)
    normed, inverse = normalize(x32)
    h = normed.astype(BF16)
    mixed = dot(h, w_qkv[...]).astype(BF16)
    q, k, v = mixed[:, :D], mixed[:, D : 2 * D], mixed[:, 2 * D :]
    q_heads = spread(q.astype(F32), [m for m in masks]).astype(BF16)
    scores = dot_nt(q_heads, k) * np.float32(HEAD ** (-0.5))
    scores = scores.reshape(HEADS, WIN, WIN) + bias[...].astype(F32)
    weighted = jnp.exp(scores)
    if allowed is not None:
        weighted = weighted * allowed[None]
    probs = weighted / jnp.sum(weighted, axis=-1, keepdims=True)
    probs = probs.reshape(HEADS * WIN, WIN)
    probs_low = probs.astype(BF16)
    o = gather_heads(dot(probs_low, v), masks).astype(BF16)
    x1 = (x32 + dot(o, w_proj[...])).astype(BF16).astype(F32)
    normed2, inverse2 = normalize(x1)
    h2 = normed2.astype(BF16)
    pre = dot(h2, w_up[...])
    cubed = pre * pre * pre
    tanh = jnp.tanh(GELU_A * (pre + GELU_B * cubed))
    u = (0.5 * pre * (1.0 + tanh)).astype(BF16)
    out = (x1 + dot(u, w_down[...])).astype(BF16)
    saved = (
        masks, normed, inverse, h, q_heads, k, v, probs, probs_low,
        o, normed2, inverse2, h2, pre, tanh, u,
    )
    return out, saved


def backward(saved, c, w_qkv, w_proj, w_up, w_down, emit):
    (
        masks, normed, inverse, h, q_heads, k, v, probs, probs_low,
        o, normed2, inverse2, h2, pre, tanh, u,
    ) = saved
    c32 = c.astype(F32)
    emit_down = dot_tn(c, u)
    du = dot_nt(c, w_down[...])
    slope = 0.5 * (1.0 + tanh) + (0.5 * GELU_A) * pre * (1.0 - tanh * tanh) * (
        1.0 + (3.0 * GELU_B) * pre * pre
    )
    dg = (du * slope).astype(BF16)
    emit_up = dot_tn(dg, h2)
    dh2 = dot_nt(dg, w_up[...])
    dx1 = c32 + normalize_back(normed2, inverse2, dh2)
    dx1_low = dx1.astype(BF16)
    emit_proj = dot_tn(dx1_low, o)
    do = dot_nt(dx1_low, w_proj[...]).astype(BF16)
    do_heads = spread(do.astype(F32), masks).astype(BF16)
    dv = dot_tn(probs_low, do_heads)
    dp = dot_nt(do_heads, v)
    inner = jnp.sum(dp * probs, axis=-1, keepdims=True)
    ds = (probs * (dp - inner) * np.float32(HEAD ** (-0.5))).astype(BF16)
    dq = gather_heads(dot(ds, k), masks)
    dk = dot_tn(ds, q_heads)
    dm = jnp.concatenate([dq, dk, dv], axis=1).astype(BF16)
    emit_qkv = dot_tn(dm, h)
    dh = dot_nt(dm, w_qkv[...])
    dx = (dx1 + normalize_back(normed, inverse, dh)).astype(BF16)
    emit(emit_qkv, emit_proj, emit_up, emit_down)
    return dx


def store_grads(ref, shares, qkv, proj, up, down):
    a, b, c, d = (g.shape[0] // shares for g in (qkv, proj, up, down))
    for s in range(shares):
        first = jnp.concatenate(
            [qkv[s * a : (s + 1) * a], proj[s * b : (s + 1) * b]], axis=0
        )
        second = up[s * c : (s + 1) * c]
        both = jnp.concatenate(
            [
                first[:, :128],
                second[:, :128],
                jnp.concatenate([first[:, 128:], second[:, 128:]], axis=1),
            ],
            axis=0,
        )
        ref[s, 0:96, :] = both.astype(BF16)
        last = down[s * d : (s + 1) * d]
        ref[s, 96:144, :] = jnp.concatenate(
            [last[:, 128 * t : 128 * (t + 1)] for t in range(6)], axis=0
        ).astype(BF16)


def plain_kernel(x, cot, w_qkv, w_proj, w_up, w_down, bias, take, y_out, piece_out):
    y, _ = forward(x[...], w_qkv, w_proj, w_up, w_down, bias, None)
    y_out[...] = y
    for k in range(3):
        piece_out[k, 0:PIECE, :] = dot(take[k], y).astype(BF16)
        piece_out[k, PIECE : 2 * PIECE, :] = dot(take[k], cot[...]).astype(BF16)


def shift_kernel(
    shares, last_row, y, cot, from_lat, from_lon, from_diag,
    w_qkv, w_proj, w_up, w_down, bias, own, own_t, put, put_t,
    nat_out, piece_out, grads_out,
):
    x = dot(own[...], y[...])
    c = dot(own[...], cot[...])
    for k, got in enumerate((from_lat, from_lon, from_diag)):
        x = x + dot(put[k], got[0:PIECE, :])
        c = c + dot(put[k], got[PIECE : 2 * PIECE, :])
    rows = lax.broadcasted_iota(jnp.int32, (WIN, WIN), 0)
    cols = lax.broadcasted_iota(jnp.int32, (WIN, WIN), 1)
    middle = WIN // 2
    apart = ((rows >= middle) ^ (cols >= middle)).astype(jnp.int32) * last_row[0]
    apart = apart + ((rows ^ cols) & 1)
    allowed = (apart == 0).astype(F32)
    result, saved = forward(x.astype(BF16), w_qkv, w_proj, w_up, w_down, bias, allowed)
    emit = functools.partial(store_grads, grads_out, shares)
    grad = backward(saved, c.astype(BF16), w_qkv, w_proj, w_up, w_down, emit)
    nat_out[0] = dot(own_t[...], result).astype(BF16)
    nat_out[1] = dot(own_t[...], grad).astype(BF16)
    for k in range(3):
        piece_out[k, 0:PIECE, :] = dot(put_t[k], result).astype(BF16)
        piece_out[k, PIECE : 2 * PIECE, :] = dot(put_t[k], grad).astype(BF16)


def final_kernel(
    shares, core, x, nat, from_lat, from_lon, from_diag,
    w_qkv, w_proj, w_up, w_down, bias, take_t, shift_grads,
    result_out, grad_out, send_out, keep_out, grads,
):
    result = nat[0].astype(F32)
    c = nat[1].astype(F32)
    for k, got in enumerate((from_lat, from_lon, from_diag)):
        result = result + dot(take_t[k], got[0:PIECE, :])
        c = c + dot(take_t[k], got[PIECE : 2 * PIECE, :])
    result_out[...] = result.astype(BF16)
    _, saved = forward(x[...], w_qkv, w_proj, w_up, w_down, bias, None)
    emit = functools.partial(store_grads, grads, shares)
    grad_out[...] = backward(
        saved, c.astype(BF16), w_qkv, w_proj, w_up, w_down, emit
    )

    @pl.when(core[0] == 0)
    def _():
        keep_out[...] = grads[...]
        send_out[...] = shift_grads[...]

    @pl.when(core[0] != 0)
    def _():
        keep_out[...] = shift_grads[...]
        send_out[...] = grads[...]


def add_kernel(a, b, out):
    out[...] = (a[...].astype(F32) + b[...].astype(F32)).astype(BF16)


def call(body, shapes, specs, name, flops, scratch=()):
    return pl.pallas_call(
        body,
        out_shape=tuple(jax.ShapeDtypeStruct(s, d) for s, d in shapes),
        in_specs=specs,
        out_specs=tuple(VMEM for _ in shapes),
        scratch_shapes=scratch,
        name=name,
        cost_estimate=pl.CostEstimate(flops=flops, bytes_accessed=4000000, transcendentals=300000),
        compiler_params=pltpu.CompilerParams(vmem_limit_bytes=48 * 1024 * 1024),
    )


def exchanged(pieces, steps):
    n_lat, n_lon = lax.axis_size("lat"), lax.axis_size("lon")
    lat = [(i, (i + steps) % n_lat) for i in range(n_lat)]
    lon = [(i, (i + steps) % n_lon) for i in range(n_lon)]
    both = [
        (j * n_lat + i, (j + steps) % n_lon * n_lat + (i + steps) % n_lat)
        for i in range(n_lat)
        for j in range(n_lon)
    ]
    return (
        lax.ppermute(pieces[2], ("lon", "lat"), both),
        lax.ppermute(pieces[1], "lon", lon),
        lax.ppermute(pieces[0], "lat", lat),
    )[::-1]


def reduced(keep, send):
    n_lon = lax.axis_size("lon")
    pair = [(i, i ^ 1) for i in range(n_lon)]
    got = lax.ppermute(send, "lon", pair)
    mine = (keep.astype(F32) + got.astype(F32)).astype(BF16)
    parts = lax.all_to_all(mine, "lat", 0, 0, tiled=True)
    share = jnp.sum(parts.astype(F32), axis=0).astype(BF16)
    for step in (8, 16, 2, 4):
        other = lax.ppermute(share, "lon", [(i, i ^ step) for i in range(n_lon)])
        share = (share.astype(F32) + other.astype(F32)).astype(BF16)
    return share, lax.ppermute(share, "lon", pair)


def unpacked(share, factor, a, b, c, d):
    share = share.astype(F32) * factor
    first = jnp.concatenate([share[0 : a + b], share[a + b + c : a + b + c + c, :64]], axis=1)
    second = jnp.concatenate([share[a + b : a + b + c], share[a + b + c : a + b + c + c, 64:]], axis=1)
    last = share[96:144].reshape(6, d, 128).transpose(1, 0, 2).reshape(d, FF)
    return first[:a].T, first[a:].T, second.T, last.T


def local(
    fields,
    cotangent,
    qkv_plain,
    proj_plain,
    up_plain,
    down_plain,
    bias_plain,
    qkv_shift,
    proj_shift,
    up_shift,
    down_shift,
    bias_shift,
):
    n_lat, n_lon = lax.axis_size("lat"), lax.axis_size("lon")
    plain = (qkv_plain, proj_plain, up_plain, down_plain, bias_plain.reshape(HEADS, WIN, WIN))
    shifted = (qkv_shift, proj_shift, up_shift, down_shift, bias_shift.reshape(HEADS, WIN, WIN))
    x = fields.reshape(WIN, D)
    cot = cotangent.reshape(WIN, D)
    own, take, put = (jnp.asarray(m, BF16) for m in (OWN, TAKE, PUT))
    own_t = jnp.asarray(OWN.T, BF16)
    take_t, put_t = (jnp.asarray(m.transpose(0, 2, 1), BF16) for m in (TAKE, PUT))
    last_row = (lax.axis_index("lat") == n_lat - 1).astype(jnp.int32).reshape(1)
    core = (lax.axis_index("lon") % 2).astype(jnp.int32).reshape(1)
    packed = (n_lat, WIN, 128)
    tokens = (WIN, D)
    moved = (3, 2 * PIECE, D)

    y, pieces = call(
        plain_kernel, ((tokens, BF16), (moved, BF16)), [VMEM] * 8, "plain", 150000000
    )(x, cot, *plain, take)
    got = exchanged(pieces, -1)
    nat, pieces, shift_grads = call(
        functools.partial(shift_kernel, n_lat),
        (((2,) + tokens, BF16), (moved, BF16), (packed, BF16)),
        [SMEM] + [VMEM] * 14,
        "shift",
        450000000,
    )(last_row, y, cot, *got, *shifted, own, own_t, put, put_t)
    got = exchanged(pieces, 1)
    result, grad_fields, send, keep = call(
        functools.partial(final_kernel, n_lat),
        ((tokens, BF16), (tokens, BF16), (packed, BF16), (packed, BF16)),
        [SMEM] + [VMEM] * 12,
        "final",
        450000000,
        (pltpu.VMEM(packed, BF16),),
    )(core, x, nat, *got, *plain, take_t, shift_grads)
    mine, other = reduced(keep, send)
    is_first = (core == 0)[:, None]
    plain_share = jnp.where(is_first, mine, other)
    shift_share = jnp.where(is_first, other, mine)
    factor = float(WIN * n_lat * n_lon) ** (-0.5)
    sizes = tuple(n // n_lat for n in (3 * D, D, FF, D))
    return (
        result.reshape(fields.shape),
        grad_fields.reshape(fields.shape),
        *unpacked(plain_share, factor, *sizes),
        *unpacked(shift_share, factor, *sizes),
    )


def solution(mesh):
    placed = (
        P("lat", "lon", None, None),
        P("lat", "lon", None, None),
        P(),
        P(),
        P(),
        P(),
        P("lat", None, None, None, None),
        P(),
        P(),
        P(),
        P(),
        P("lat", None, None, None, None),
    )
    return jax.shard_map(
        local,
        mesh=mesh,
        in_specs=placed,
        out_specs=(
            P("lat", "lon", None, None),
            P("lat", "lon", None, None),
            P(None, "lat"),
            P(None, "lat"),
            P(None, "lat"),
            P(None, "lat"),
            P(None, "lat"),
            P(None, "lat"),
            P(None, "lat"),
            P(None, "lat"),
        ),
        check_vma=False,
    )
```

time: 600 us -> 151 us (0.25)
  waiting for transfers between devices: 433 us -> 27 us
  local copies, waits for them, and re-layouts: 62 us -> 18.5 us
  matrix products: 29.7 us -> 0 us
  blocking collectives: 0 us -> 28.4 us
  starting transfers between devices: 42.7 us -> 60.6 us
  between operations: 15.3 us -> 0.99 us
  other arithmetic: 16.1 us -> 4.1 us
  Pallas kernels: 0 us -> 9.23 us
    psum x1 -> x0, waiting for transfers between devices: 343 us -> none  [reduce_all(): lax.psum(shares[0].astype(jnp.bfloat16), 'lon').astype(jnp.float32)]
    reduce_scatter x1 -> x0, waiting for transfers between devices: 80.4 us -> none  [one_scatter(): lax.psum_scatter(lines, axis, tiled=True).reshape(-1)]
    all_to_all x0 -> x1, blocking collectives: none -> 28.4 us  [reduced(): parts = lax.all_to_all(mine, 'lat', 0, 0, tiled=True)]
    dot_general x34 -> x0, matrix products: 27.7 us -> none  [the longest x2 3.43 us: block_backward(): jnp.einsum('bnhqk,bnqhd->bnkhd', grad_scores, query_part, preferred_eleme...]
    reshape x21 -> x4, local copies, waits for them, and re-layouts: 26.2 us -> 3.26 us  [the longest x1 0.96 us: local(): x = fields.reshape(WIN, D)]
    ppermute x8 -> x12, starting transfers between devices: 42.7 us -> 60.6 us  [the longest x2 15.1 us: exchanged(): lax.ppermute(pieces[2], ('lon', 'lat'), both)]
    ppermute x8 -> x12, waiting for transfers between devices: 9.09 us -> 27 us  [the longest x4 17.8 us: reduced(): other = lax.ppermute(share, 'lon', [(i, i ^ step) for i in range(n_lon)])]
    pallas_call x0 -> x3, Pallas kernels: none -> 9.23 us  [the longest x1 3.88 us: local(): call(functools.partial(shift_kernel, n_lat), (((2,) + tokens, BF16), (mov...]
  transfers between devices with their start and end apart: 10 -> 12, of which waited for: 4 -> 7; matrix products, arithmetic and copies ran while one was open for 5% -> 1% of each run, Pallas kernels for 0% -> 0%
where the time goes in v1:
time: 151 us; the launch traced here: 149 us
  starting transfers between devices  60.6 us (40%)
  blocking collectives  28.4 us (19%)
  waiting for transfers between devices  27 us (18%)
  local copies, waits for them, and re-layouts  18.5 us (12%)
  Pallas kernels  9.23 us (6%)
  other arithmetic  4.1 us (3%)
    all_to_all x1, blocking collectives, reduced(): parts = lax.all_to_all(mine, 'lat', 0, 0, tiled=True)  28.4 us
    ppermute x4, waiting for transfers between devices, reduced(): other = lax.ppermute(share, 'lon', [(i, i ^ step) for i in range(n_lon)])  17.8 us
    ppermute x2, starting transfers between devices, exchanged(): lax.ppermute(pieces[2], ('lon', 'lat'), both)  15.1 us
    unnamed x50, local copies, waits for them, and re-layouts  14.6 us
    ppermute x2, starting transfers between devices, exchanged(): lax.ppermute(pieces[0], 'lat', lat)  12 us
    ppermute x4, starting transfers between devices, reduced(): other = lax.ppermute(share, 'lon', [(i, i ^ step) for i in range(n_lon)])  10.7 us
    ppermute x1, starting transfers between devices, reduced(): return (share, lax.ppermute(share, 'lon', pair))  9.36 us
    ppermute x1, starting transfers between devices, reduced(): got = lax.ppermute(send, 'lon', pair)  6.78 us
  transfers between devices with their start and end apart: 12, of which 7 were waited for; matrix products, arithmetic and copies ran while one was open for 1% of the time, Pallas kernels for 0%

profile of v1, /device:TPU:1, one launch (start us, length us, event | category | flops | bytes accessed | tf_op | source)
XLA Modules:
  0.0 148.9 jit_solution(5708057470882762967)
XLA Ops:
  0.7 1.2 copy.28.w_down
  1.9 1.0 reshape.60.x
  2.8 1.0 reshape.63.cot
  3.9 0.9 copy-done.4
  4.7 0.8 copy-done.16
  5.6 1.8 %plain.1 = (bf16[144,192]{1,0:T(8,128)(2,1)S(1)}, bf16[3,80,192]{2,1,0:T(8,128)(2,1)S(1)}) custom-call(bf16[144,192]{1,0:T(8,128)(2,1)S(1)} %reshape.60.x, bf16[144,192]{1,0:T(8,128)(2,1)S(1)} %reshape.63.cot, bf16[192,576]{1,0:T(8,128)(2,1)S(1)} %copy-done.2, bf16[192,192]{1,0:T(8,128)(2,1)S(1)} %copy-done.4, bf16[192,768]{1,0:T(8,128)(2,1)S(1)} %copy-done.1, ...), custom_call_target="tpu_custom_call" | custom-call | flops 150000000 | bytes 4000000 | tf_op jit(solution)/shard_map/plain/pallas_call | solution.py:334
  7.5 9.7 %collective-permute-start = (bf16[80,192]{1,0:T(8,128)(2,1)S(1)}, bf16[80,192]{1,0:T(8,128)(2,1)S(1)}, u32[]{:S(2)}, u32[]{:S(2)}) collective-permute-start(bf16[80,192]{1,0:T(8,128)(2,1)S(1)} %get-tuple-element.33), channel_id=1, source_target_pairs={{0,23},{1,0},{2,1},{3,2},{4,3},{5,4},{6,5},{7,6},{8,7},{9,8},{10,9... | collective-permute-start | bytes 92168 | tf_op jit(solution)/shard_map/ppermute | solution.py:281
  17.1 4.8 %collective-permute-start.1 = (bf16[80,192]{1,0:T(8,128)(2,1)S(1)}, bf16[80,192]{1,0:T(8,128)(2,1)S(1)}, u32[]{:S(2)}, u32[]{:S(2)}) collective-permute-start(bf16[80,192]{1,0:T(8,128)(2,1)S(1)} %get-tuple-element.32), channel_id=1, source_target_pairs={{0,744},{24,0},{48,24},{72,48},{96,72},{120,96},{144,120},{168,144... | collective-permute-start | bytes 92168 | tf_op jit(solution)/shard_map/ppermute | solution.py:280
  21.9 13.2 %collective-permute-start.2 = (bf16[80,192]{1,0:T(8,128)(2,1)S(1)}, bf16[80,192]{1,0:T(8,128)(2,1)S(1)}, u32[]{:S(2)}, u32[]{:S(2)}) collective-permute-start(bf16[80,192]{1,0:T(8,128)(2,1)S(1)} %get-tuple-element.31), channel_id=1, source_target_pairs={{0,767},{24,23},{48,47},{72,71},{96,95},{120,119},{144,143},{168,1... | collective-permute-start | bytes 92168 | tf_op jit(solution)/shard_map/ppermute | solution.py:279
  35.9 0.6 copy-done.19
  36.6 0.6 copy-done.21
  37.2 1.0 copy-done.6
  38.2 0.9 copy-done.7
  39.1 0.9 copy-done.9
  40.0 0.9 copy-done.10
  40.9 0.9 copy-done.11
  41.8 0.9 copy-done.12
  42.7 0.9 copy-done.14
  43.5 0.8 copy-done.18
  44.3 0.8 copy-done.20
  45.1 0.8 copy-done.22
  45.9 3.9 %shift.1 = (bf16[2,144,192]{2,1,0:T(8,128)(2,1)S(1)}, bf16[3,80,192]{2,1,0:T(8,128)(2,1)S(1)}, bf16[24,144,128]{2,1,0:T(8,128)(2,1)S(1)}) custom-call(s32[1]{0:T(128)} %bitcast.1.last_row, bf16[144,192]{1,0:T(8,128)(2,1)S(1)} %copy-done.14, bf16[144,192]{1,0:T(8,128)(2,1)S(1)} %reshape.63.cot, bf16[80,192]{1,0:T(8,128)(2,1)S(1)} %copy-done.18, ...), custom_call_target="tpu_custom_call" | custom-call | flops 450000000 | bytes 4000000 | tf_op jit(solution)/shard_map/shift/pallas_call | solution.py:338
  49.8 2.3 %collective-permute-start.3 = (bf16[80,192]{1,0:T(8,128)(2,1)S(1)}, bf16[80,192]{1,0:T(8,128)(2,1)S(1)}, u32[]{:S(2)}, u32[]{:S(2)}) collective-permute-start(bf16[80,192]{1,0:T(8,128)(2,1)S(1)} %get-tuple-element.30), channel_id=1, source_target_pairs={{0,1},{1,2},{2,3},{3,4},{4,5},{5,6},{6,7},{7,8},{8,9},{9,10},{10,1... | collective-permute-start | bytes 92168 | tf_op jit(solution)/shard_map/ppermute | solution.py:281
  52.1 1.9 %collective-permute-start.4 = (bf16[80,192]{1,0:T(8,128)(2,1)S(1)}, bf16[80,192]{1,0:T(8,128)(2,1)S(1)}, u32[]{:S(2)}, u32[]{:S(2)}) collective-permute-start(bf16[80,192]{1,0:T(8,128)(2,1)S(1)} %get-tuple-element.29), channel_id=1, source_target_pairs={{0,24},{24,48},{48,72},{72,96},{96,120},{120,144},{144,168},{168,1... | collective-permute-start | bytes 92168 | tf_op jit(solution)/shard_map/ppermute | solution.py:280
  54.0 1.9 %collective-permute-start.5 = (bf16[80,192]{1,0:T(8,128)(2,1)S(1)}, bf16[80,192]{1,0:T(8,128)(2,1)S(1)}, u32[]{:S(2)}, u32[]{:S(2)}) collective-permute-start(bf16[80,192]{1,0:T(8,128)(2,1)S(1)} %get-tuple-element.28), channel_id=1, source_target_pairs={{0,25},{24,49},{48,73},{72,97},{96,121},{120,145},{144,169},{168,1... | collective-permute-start | bytes 92168 | tf_op jit(solution)/shard_map/ppermute | solution.py:279
  56.0 1.6 %collective-permute-done.3.from_lat = bf16[80,192]{1,0:T(8,128)(2,1)S(1)} collective-permute-done((bf16[80,192]{1,0:T(8,128)(2,1)S(1)}, bf16[80,192]{1,0:T(8,128)(2,1)S(1)}, u32[]{:S(2)}, u32[]{:S(2)}) %collective-permute-start.3) | collective-permute-done | bytes 30752 | tf_op jit(solution)/shard_map/ppermute | solution.py:281
  57.5 5.6 %collective-permute-done.5.from_diag = bf16[80,192]{1,0:T(8,128)(2,1)S(1)} collective-permute-done((bf16[80,192]{1,0:T(8,128)(2,1)S(1)}, bf16[80,192]{1,0:T(8,128)(2,1)S(1)}, u32[]{:S(2)}, u32[]{:S(2)}) %collective-permute-start.5) | collective-permute-done | bytes 30752 | tf_op jit(solution)/shard_map/ppermute | solution.py:279
  63.1 0.9 copy-done.8
  64.0 3.5 %final.1 = (bf16[144,192]{1,0:T(8,128)(2,1)S(1)}, bf16[144,192]{1,0:T(8,128)(2,1)S(1)}, bf16[24,144,128]{2,1,0:T(8,128)(2,1)S(1)}, bf16[24,144,128]{2,1,0:T(8,128)(2,1)S(1)}) custom-call(s32[1]{0:T(128)} %bitcast.core, bf16[144,192]{1,0:T(8,128)(2,1)S(1)} %reshape.60.x, bf16[2,144,192]{2,1,0:T(8,128)(2,1)S(1)} %get-tuple-element.21.nat, ...), custom_call_target="tpu_custom_call" | custom-call | flops 450000000 | bytes 4000000 | tf_op jit(solution)/shard_map/final/pallas_call | solution.py:346
  67.5 6.8 %collective-permute-start.6 = (bf16[24,144,128]{2,1,0:T(8,128)(2,1)S(1)}, bf16[24,144,128]{2,1,0:T(8,128)(2,1)S(1)}, u32[]{:S(2)}, u32[]{:S(2)}) collective-permute-start(bf16[24,144,128]{2,1,0:T(8,128)(2,1)S(1)} %get-tuple-element.27), channel_id=1, source_target_pairs={{0,24},{24,0},{48,72},{72,48},{96,120},{120,96},{144,168},{168,144... | collective-permute-start | bytes 2654216 | tf_op jit(solution)/shard_map/ppermute | solution.py:288
  74.3 2.0 %collective-permute-done.6 = bf16[24,144,128]{2,1,0:T(8,128)(2,1)S(1)} collective-permute-done((bf16[24,144,128]{2,1,0:T(8,128)(2,1)S(1)}, bf16[24,144,128]{2,1,0:T(8,128)(2,1)S(1)}, u32[]{:S(2)}, u32[]{:S(2)}) %collective-permute-start.6) | collective-permute-done | bytes 884768 | tf_op jit(solution)/shard_map/ppermute | solution.py:288
  76.6 28.4 %all_to_all.5 = bf16[24,144,128]{2,1,0:T(8,128)(2,1)S(1)} all-to-all(bf16[24,144,128]{2,1,0:T(8,128)(2,1)S(1)} %add_convert_fusion), channel_id=1, replica_groups=mesh['lon'=32,'lat'=24] {'lat'}, dimensions={0} | all-to-all | bytes 1769472 | tf_op jit(solution)/shard_map/all_to_all | solution.py:290
  105.2 1.9 %collective-permute-start.7 = (bf16[144,128]{1,0:T(8,128)(2,1)S(1)}, bf16[144,128]{1,0:T(8,128)(2,1)S(1)}, u32[]{:S(2)}, u32[]{:S(2)}) collective-permute-start(bf16[144,128]{1,0:T(8,128)(2,1)S(1)} %reduce_sum.12), channel_id=1, source_target_pairs={{0,192},{24,216},{48,240},{72,264},{96,288},{120,312},{144,336},{1... | collective-permute-start | bytes 110600 | tf_op jit(solution)/shard_map/ppermute | solution.py:293
  107.1 2.8 %collective-permute-done.7 = bf16[144,128]{1,0:T(8,128)(2,1)S(1)} collective-permute-done((bf16[144,128]{1,0:T(8,128)(2,1)S(1)}, bf16[144,128]{1,0:T(8,128)(2,1)S(1)}, u32[]{:S(2)}, u32[]{:S(2)}) %collective-permute-start.7) | collective-permute-done | bytes 36896 | tf_op jit(solution)/shard_map/ppermute | solution.py:293
  109.9 1.9 %collective-permute-start.8 = (bf16[144,128]{1,0:T(8,128)(2,1)S(1)}, bf16[144,128]{1,0:T(8,128)(2,1)S(1)}, u32[]{:S(2)}, u32[]{:S(2)}) collective-permute-start(bf16[144,128]{1,0:T(8,128)(2,1)S(1)} %add_convert_fusion.4), channel_id=1, source_target_pairs={{0,384},{24,408},{48,432},{72,456},{96,480},{120,504},{144,528},{1... | collective-permute-start | bytes 110600 | tf_op jit(solution)/shard_map/ppermute | solution.py:293
  111.8 4.3 %collective-permute-done.8 = bf16[144,128]{1,0:T(8,128)(2,1)S(1)} collective-permute-done((bf16[144,128]{1,0:T(8,128)(2,1)S(1)}, bf16[144,128]{1,0:T(8,128)(2,1)S(1)}, u32[]{:S(2)}, u32[]{:S(2)}) %collective-permute-start.8) | collective-permute-done | bytes 36896 | tf_op jit(solution)/shard_map/ppermute | solution.py:293
  116.1 1.9 %collective-permute-start.9 = (bf16[144,128]{1,0:T(8,128)(2,1)S(1)}, bf16[144,128]{1,0:T(8,128)(2,1)S(1)}, u32[]{:S(2)}, u32[]{:S(2)}) collective-permute-start(bf16[144,128]{1,0:T(8,128)(2,1)S(1)} %add_convert_fusion.3), channel_id=1, source_target_pairs={{0,48},{24,72},{48,0},{72,24},{96,144},{120,168},{144,96},{168,120... | collective-permute-start | bytes 110600 | tf_op jit(solution)/shard_map/ppermute | solution.py:293
  118.0 4.6 %collective-permute-done.9 = bf16[144,128]{1,0:T(8,128)(2,1)S(1)} collective-permute-done((bf16[144,128]{1,0:T(8,128)(2,1)S(1)}, bf16[144,128]{1,0:T(8,128)(2,1)S(1)}, u32[]{:S(2)}, u32[]{:S(2)}) %collective-permute-start.9) | collective-permute-done | bytes 36896 | tf_op jit(solution)/shard_map/ppermute | solution.py:293
  122.6 4.9 %collective-permute-start.10 = (bf16[144,128]{1,0:T(8,128)(2,1)S(1)}, bf16[144,128]{1,0:T(8,128)(2,1)S(1)}, u32[]{:S(2)}, u32[]{:S(2)}) collective-permute-start(bf16[144,128]{1,0:T(8,128)(2,1)S(1)} %add_convert_fusion.2), channel_id=1, source_target_pairs={{0,96},{24,120},{48,144},{72,168},{96,0},{120,24},{144,48},{168,72... | collective-permute-start | bytes 110600 | tf_op jit(solution)/shard_map/ppermute | solution.py:293
  127.6 6.2 %collective-permute-done.10 = bf16[144,128]{1,0:T(8,128)(2,1)S(1)} collective-permute-done((bf16[144,128]{1,0:T(8,128)(2,1)S(1)}, bf16[144,128]{1,0:T(8,128)(2,1)S(1)}, u32[]{:S(2)}, u32[]{:S(2)}) %collective-permute-start.10) | collective-permute-done | bytes 36896 | tf_op jit(solution)/shard_map/ppermute | solution.py:293
  133.7 9.4 %collective-permute-start.11 = (bf16[144,128]{1,0:T(8,128)(2,1)S(1)}, bf16[144,128]{1,0:T(8,128)(2,1)S(1)}, u32[]{:S(2)}, u32[]{:S(2)}) collective-permute-start(bf16[144,128]{1,0:T(8,128)(2,1)S(1)} %add_convert_fusion.1), channel_id=1, source_target_pairs={{0,24},{24,0},{48,72},{72,48},{96,120},{120,96},{144,168},{168,144... | collective-permute-start | bytes 110600 | tf_op jit(solution)/shard_map/ppermute | solution.py:295
  143.1 0.7 reshape.66
  143.8 0.7 reshape.67
  145.2 0.6 fusion.1
  145.8 0.6 slice_bitcast_fusion.6
  147.0 0.6 fusion.3
  147.6 0.6 maximum_bitcast_fusion.1
  148.2 0.6 maximum_bitcast_fusion
  (52 shorter events, 2.6 us)
Async XLA Ops:
  0.6 3.2 %copy-start = (bf16[1,1,6,144,144]{4,3,2,1,0:T(8,128)(2,1)S(1)}, bf16[1,1,6,144,144]{4,3,2,1,0:T(8,128)(2,1)}, u32[]{:S(2)}) copy-start(bf16[1,1,6,144,144]{4,3,2,1,0:T(8,128)(2,1)} %param.24) | copy-start | bytes 746500
  0.7 3.2 %copy-start.2 = (bf16[192,576]{1,0:T(8,128)(2,1)S(1)}, bf16[192,576]{1,0:T(8,128)(2,1)}, u32[]{:S(2)}) copy-start(bf16[192,576]{1,0:T(8,128)(2,1)} %w_qkv.5) | copy-start | bytes 663556
  0.7 3.2 %copy-start.1 = (bf16[192,768]{1,0:T(8,128)(2,1)S(1)}, bf16[192,768]{1,0:T(8,128)(2,1)}, u32[]{:S(2)}) copy-start(bf16[192,768]{1,0:T(8,128)(2,1)} %w_up.5) | copy-start | bytes 884740
  3.8 0.9 copy-start.4
  4.7 0.8 copy-start.16
  5.6 29.6 %copy-start.23 = (bf16[768,192]{0,1:T(8,128)(2,1)S(1)}, bf16[768,192]{0,1:T(8,128)(2,1)}, u32[]{:S(2)}) copy-start(bf16[768,192]{0,1:T(8,128)(2,1)} %param.28) | copy-start | bytes 884740
  7.4 27.7 %copy-start.13 = (bf16[144,192]{1,0:T(8,128)(2,1)}, bf16[144,192]{1,0:T(8,128)(2,1)S(1)}, u32[]{:S(2)}) copy-start(bf16[144,192]{1,0:T(8,128)(2,1)S(1)} %get-tuple-element.19.y) | copy-start | bytes 165892
  7.4 29.8 %copy-start.3 = (bf16[1,1,6,144,144]{4,3,2,1,0:T(8,128)(2,1)S(1)}, bf16[1,1,6,144,144]{4,3,2,1,0:T(8,128)(2,1)}, u32[]{:S(2)}) copy-start(bf16[1,1,6,144,144]{4,3,2,1,0:T(8,128)(2,1)} %param.29) | copy-start | bytes 746500
  7.4 29.7 %copy-start.15 = (bf16[3,40,144]{2,1,0:T(8,128)(2,1)S(1)}, bf16[3,40,144]{2,1,0:T(8,128)(2,1)}, u32[]{:S(2)}) copy-start(bf16[3,40,144]{2,1,0:T(8,128)(2,1)} %constant.45.clone.put_t) | copy-start | bytes 103684
  7.5 27.8 %collective-permute-start = (bf16[80,192]{1,0:T(8,128)(2,1)S(1)}, bf16[80,192]{1,0:T(8,128)(2,1)S(1)}, u32[]{:S(2)}, u32[]{:S(2)}) collective-permute-start(bf16[80,192]{1,0:T(8,128)(2,1)S(1)} %get-tuple-element.33), channel_id=1, source_target_pairs={{0,23},{1,0},{2,1},{3,2},{4,3},{5,4},{6,5},{7,6},{8,7},{9,8},{10,9... | collective-permute-start | bytes 92168 | tf_op jit(solution)/shard_map/ppermute | solution.py:281
  17.1 18.8 %collective-permute-start.1 = (bf16[80,192]{1,0:T(8,128)(2,1)S(1)}, bf16[80,192]{1,0:T(8,128)(2,1)S(1)}, u32[]{:S(2)}, u32[]{:S(2)}) collective-permute-start(bf16[80,192]{1,0:T(8,128)(2,1)S(1)} %get-tuple-element.32), channel_id=1, source_target_pairs={{0,744},{24,0},{48,24},{72,48},{96,72},{120,96},{144,120},{168,144... | collective-permute-start | bytes 92168 | tf_op jit(solution)/shard_map/ppermute | solution.py:280
  21.9 14.6 %collective-permute-start.2 = (bf16[80,192]{1,0:T(8,128)(2,1)S(1)}, bf16[80,192]{1,0:T(8,128)(2,1)S(1)}, u32[]{:S(2)}, u32[]{:S(2)}) collective-permute-start(bf16[80,192]{1,0:T(8,128)(2,1)S(1)} %get-tuple-element.31), channel_id=1, source_target_pairs={{0,767},{24,23},{48,47},{72,71},{96,95},{120,119},{144,143},{168,1... | collective-permute-start | bytes 92168 | tf_op jit(solution)/shard_map/ppermute | solution.py:279
  35.3 0.6 copy-start.17
  35.9 0.6 copy-start.19
  36.6 0.6 copy-start.21
  37.2 1.0 copy-start.6
  38.2 0.9 copy-start.7
  39.1 0.9 copy-start.9
  40.0 0.9 copy-start.10
  40.9 0.9 copy-start.11
  41.8 0.9 copy-start.12
  42.7 0.9 copy-start.14
  43.5 0.8 copy-start.18
  44.3 0.8 copy-start.20
  45.1 0.8 copy-start.22
  45.9 17.2 %copy-start.5 = (bf16[192,192]{1,0:T(8,128)(2,1)S(1)}, bf16[192,192]{1,0:T(8,128)(2,1)}, u32[]{:S(2)}) copy-start(bf16[192,192]{1,0:T(8,128)(2,1)} %w_proj.5) | copy-start | bytes 221188
  49.8 7.8 %collective-permute-start.3 = (bf16[80,192]{1,0:T(8,128)(2,1)S(1)}, bf16[80,192]{1,0:T(8,128)(2,1)S(1)}, u32[]{:S(2)}, u32[]{:S(2)}) collective-permute-start(bf16[80,192]{1,0:T(8,128)(2,1)S(1)} %get-tuple-element.30), channel_id=1, source_target_pairs={{0,1},{1,2},{2,3},{3,4},{4,5},{5,6},{6,7},{7,8},{8,9},{9,10},{10,1... | collective-permute-start | bytes 92168 | tf_op jit(solution)/shard_map/ppermute | solution.py:281
  52.1 5.4 %collective-permute-start.4 = (bf16[80,192]{1,0:T(8,128)(2,1)S(1)}, bf16[80,192]{1,0:T(8,128)(2,1)S(1)}, u32[]{:S(2)}, u32[]{:S(2)}) collective-permute-start(bf16[80,192]{1,0:T(8,128)(2,1)S(1)} %get-tuple-element.29), channel_id=1, source_target_pairs={{0,24},{24,48},{48,72},{72,96},{96,120},{120,144},{144,168},{168,1... | collective-permute-start | bytes 92168 | tf_op jit(solution)/shard_map/ppermute | solution.py:280
  54.0 9.1 %collective-permute-start.5 = (bf16[80,192]{1,0:T(8,128)(2,1)S(1)}, bf16[80,192]{1,0:T(8,128)(2,1)S(1)}, u32[]{:S(2)}, u32[]{:S(2)}) collective-permute-start(bf16[80,192]{1,0:T(8,128)(2,1)S(1)} %get-tuple-element.28), channel_id=1, source_target_pairs={{0,25},{24,49},{48,73},{72,97},{96,121},{120,145},{144,169},{168,1... | collective-permute-start | bytes 92168 | tf_op jit(solution)/shard_map/ppermute | solution.py:279
  63.1 0.9 copy-start.8
  67.5 8.8 %collective-permute-start.6 = (bf16[24,144,128]{2,1,0:T(8,128)(2,1)S(1)}, bf16[24,144,128]{2,1,0:T(8,128)(2,1)S(1)}, u32[]{:S(2)}, u32[]{:S(2)}) collective-permute-start(bf16[24,144,128]{2,1,0:T(8,128)(2,1)S(1)} %get-tuple-element.27), channel_id=1, source_target_pairs={{0,24},{24,0},{48,72},{72,48},{96,120},{120,96},{144,168},{168,144... | collective-permute-start | bytes 2654216 | tf_op jit(solution)/shard_map/ppermute | solution.py:288
  105.2 4.7 %collective-permute-start.7 = (bf16[144,128]{1,0:T(8,128)(2,1)S(1)}, bf16[144,128]{1,0:T(8,128)(2,1)S(1)}, u32[]{:S(2)}, u32[]{:S(2)}) collective-permute-start(bf16[144,128]{1,0:T(8,128)(2,1)S(1)} %reduce_sum.12), channel_id=1, source_target_pairs={{0,192},{24,216},{48,240},{72,264},{96,288},{120,312},{144,336},{1... | collective-permute-start | bytes 110600 | tf_op jit(solution)/shard_map/ppermute | solution.py:293
  109.9 6.2 %collective-permute-start.8 = (bf16[144,128]{1,0:T(8,128)(2,1)S(1)}, bf16[144,128]{1,0:T(8,128)(2,1)S(1)}, u32[]{:S(2)}, u32[]{:S(2)}) collective-permute-start(bf16[144,128]{1,0:T(8,128)(2,1)S(1)} %add_convert_fusion.4), channel_id=1, source_target_pairs={{0,384},{24,408},{48,432},{72,456},{96,480},{120,504},{144,528},{1... | collective-permute-start | bytes 110600 | tf_op jit(solution)/shard_map/ppermute | solution.py:293
  116.1 6.5 %collective-permute-start.9 = (bf16[144,128]{1,0:T(8,128)(2,1)S(1)}, bf16[144,128]{1,0:T(8,128)(2,1)S(1)}, u32[]{:S(2)}, u32[]{:S(2)}) collective-permute-start(bf16[144,128]{1,0:T(8,128)(2,1)S(1)} %add_convert_fusion.3), channel_id=1, source_target_pairs={{0,48},{24,72},{48,0},{72,24},{96,144},{120,168},{144,96},{168,120... | collective-permute-start | bytes 110600 | tf_op jit(solution)/shard_map/ppermute | solution.py:293
  122.6 11.1 %collective-permute-start.10 = (bf16[144,128]{1,0:T(8,128)(2,1)S(1)}, bf16[144,128]{1,0:T(8,128)(2,1)S(1)}, u32[]{:S(2)}, u32[]{:S(2)}) collective-permute-start(bf16[144,128]{1,0:T(8,128)(2,1)S(1)} %add_convert_fusion.2), channel_id=1, source_target_pairs={{0,96},{24,120},{48,144},{72,168},{96,0},{120,24},{144,48},{168,72... | collective-permute-start | bytes 110600 | tf_op jit(solution)/shard_map/ppermute | solution.py:293
  133.7 10.7 %collective-permute-start.11 = (bf16[144,128]{1,0:T(8,128)(2,1)S(1)}, bf16[144,128]{1,0:T(8,128)(2,1)S(1)}, u32[]{:S(2)}, u32[]{:S(2)}) collective-permute-start(bf16[144,128]{1,0:T(8,128)(2,1)S(1)} %add_convert_fusion.1), channel_id=1, source_target_pairs={{0,24},{24,0},{48,72},{72,48},{96,120},{120,96},{144,168},{168,144... | collective-permute-start | bytes 110600 | tf_op jit(solution)/shard_map/ppermute | solution.py:295
